TPU v7x, 32 devices: a whole 2x2x4 slice. The times are simulated.
32 devices in a mesh: fem: 4 (over y, x), bem: 8 (over z, core).
Axes of the slice: x: 2, y: 2, z: 4, core: 2. Of those that a mesh axis runs over, the one named last changes fastest.
Arguments:
- fem_field: float32 [32, 64, 32, 128], P('fem', 'bem'), may hold values from -6 to 6
- fem_source: float32 [32, 64, 32, 128], P('fem', 'bem'), may hold values from -6 to 6
- reaction: float32 [32, 64, 32], P('fem', 'bem'), may hold values from 0.5 to 3
- bem_density: float32 [128, 8192], P(None, 'bem'), may hold values from -6 to 6
- bem_source: float32 [128, 8192], P(None, 'bem'), may hold values from -6 to 6
- bem_diagonal: float32 [8192], P('bem'), may hold values from 2 to 6
- near_blocks: bfloat16 [16, 48, 512, 512], P('bem', 'fem'), may hold values from -0.0390625 to 0.0390625
- near_pairs: int32 [16, 48], P('bem'), may hold values from 0 to 15, as said below
- low_left: bfloat16 [16, 32, 512], P('bem'), may hold values from -1 to 1
- low_right: bfloat16 [16, 32, 512], replicated, may hold values from -0.25 to 0.25
- centers: float32 [16, 3], replicated, may hold values from 0 to 4
- trace_cell: int32 [8192], P(('fem', 'bem')), may hold values from 0 to 2047
- trace_bank: int32 [8192, 1], P(('fem', 'bem')), may hold values from 0 to 7; in each aligned block of 256 rows (0 to 255, 256 to 511, ...) at most 32 rows name the same one
- trace_row: int32 [8192], P(('fem', 'bem')), may hold values from 0 to 1023
Outputs:
- fem_out: float32 [32, 64, 32, 128], P('fem', 'bem')
- bem_out: float32 [128, 8192], P('fem', 'bem')
Inputs may be any that keep to these rules, and one draw needn't show every extreme that they name: `trace_bank`: among the 256 slots of one device no bem index is named more than 32 times, and some device names some index exactly 32 times. Panel p's near-field source panels are held by bem indices within two of p's own, counted around the bem axis: near_pairs[p, k] // 2 - p // 2 is -2, -1, 0, 1 or 2 modulo 8.
All inputs are finite; a program needn't handle non-finite values.
Results may differ from a plain program's by a relative error of at most 0.0028.
Values may be sent and summed in bfloat16 or wider, within the bound.
A program may use at most 128 MiB of HBM per device.

v0:
```python
import jax
import jax.numpy as jnp
from jax import lax
from jax.experimental import pallas as pl
from jax.experimental.pallas import tpu as pltpu
from jax.sharding import PartitionSpec as P

CAP = 32
ITERS = 3


HIGHEST = lax.Precision.HIGHEST


def faces(x, axis, dim):
    size, length = (lax.axis_size(axis), x.shape[dim])
    up = [(i, (i + 1) % size) for i in range(size - 1)]
    down = [(j, i) for i, j in up]
    last = lax.slice_in_dim(x, length - 1, length, axis=dim).astype(jnp.bfloat16)
    initial = lax.slice_in_dim(x, 0, 1, axis=dim).astype(jnp.bfloat16)
    return lax.ppermute(last, axis, up), lax.ppermute(initial, axis, down)


def neighbour_sum(state, before_x, after_x, before_y, after_y):
    wide_x = jnp.concatenate(
        [before_x.astype(jnp.float32), state, after_x.astype(jnp.float32)], axis=0
    )
    wide_y = jnp.concatenate(
        [before_y.astype(jnp.float32), state, after_y.astype(jnp.float32)], axis=1
    )
    wide_z = jnp.pad(state, ((0, 0), (0, 0), (1, 1), (0, 0)))
    beside = wide_x[2:] + wide_x[:-2] + wide_y[:, 2:] + wide_y[:, :-2]
    return beside + wide_z[:, :, 2:] + wide_z[:, :, :-2]


def near_kernel(pairs_ref, x_ref, blocks_ref, init_ref, out_ref, acc_ref):
    p, k = pl.program_id(0), pl.program_id(1)

    @pl.when(k == 0)
    def _():
        acc_ref[...] = init_ref[...]

    acc_ref[...] += jnp.dot(
        x_ref[pairs_ref[p, k]], blocks_ref[0, 0], preferred_element_type=jnp.float32
    )

    @pl.when(k == pl.num_programs(1) - 1)
    def _():
        out_ref[...] = acc_ref[...].astype(out_ref.dtype)


def near_apply(pairs, x, blocks, init):
    panels, group, rows, cols = blocks.shape
    exc = x.shape[1]
    return pl.pallas_call(
        near_kernel,
        out_shape=jax.ShapeDtypeStruct((exc, panels * cols), jnp.bfloat16),
        grid_spec=pltpu.PrefetchScalarGridSpec(
            num_scalar_prefetch=1,
            grid=(panels, group),
            in_specs=[
                pl.BlockSpec(x.shape, lambda p, k, pairs: (0, 0, 0)),
                pl.BlockSpec((1, 1, rows, cols), lambda p, k, pairs: (p, k, 0, 0)),
                pl.BlockSpec((exc, cols), lambda p, k, pairs: (0, p)),
            ],
            out_specs=pl.BlockSpec((exc, cols), lambda p, k, pairs: (0, p)),
            scratch_shapes=[pltpu.VMEM((exc, cols), jnp.float32)],
        ),
        cost_estimate=pl.CostEstimate(
            flops=2 * exc * blocks.size, bytes_accessed=2 * blocks.size, transcendentals=0
        ),
        compiler_params=pltpu.CompilerParams(
            dimension_semantics=("arbitrary", "arbitrary"), vmem_limit_bytes=24 << 20
        ),
        name="near",
    )(pairs, x, blocks, init)


def pick_kernel(node_ref, x_ref, out_ref):
    panels, exc, rows = x_ref.shape
    slots = node_ref.shape[0]
    node = node_ref[...]
    lanes = lax.broadcasted_iota(jnp.int32, (slots, rows), 1)

    def step(q, acc):
        hot = jnp.where(lanes + q * rows == node, 1.0, 0.0).astype(jnp.bfloat16)
        return acc + lax.dot_general(
            hot, x_ref[q], (((1,), (1,)), ((), ())), preferred_element_type=jnp.float32
        )

    acc = lax.fori_loop(0, panels, step, jnp.zeros((slots, exc), jnp.float32))
    out_ref[...] = acc.astype(out_ref.dtype)


def pick_nodes(node, x):
    slots = node.shape[0]
    return pl.pallas_call(
        pick_kernel,
        out_shape=jax.ShapeDtypeStruct((slots, x.shape[1]), jnp.bfloat16),
        cost_estimate=pl.CostEstimate(
            flops=2 * slots * x.size, bytes_accessed=2 * x.size, transcendentals=0
        ),
        compiler_params=pltpu.CompilerParams(vmem_limit_bytes=24 << 20),
        name="pick",
    )(node, x)


def shards(
    fem_field,
    fem_source,
    reaction,
    bem_density,
    bem_source,
    bem_diagonal,
    near_blocks,
    near_pairs,
    low_left,
    low_right,
    centers,
    trace_cell,
    trace_bank,
    trace_row,
):
    fem_count = lax.axis_size("fem")
    bem_count = lax.axis_size("bem")
    fem_rank = lax.axis_index("fem")
    bem_rank = lax.axis_index("bem")
    excitations, local_rows = bem_density.shape
    share_cols = excitations // fem_count
    local_panels = near_blocks.shape[0]
    group_size = near_blocks.shape[1]
    panel_rows = near_blocks.shape[2]
    panel_total = low_right.shape[0]
    cell_total = reaction.size
    slot_total = trace_cell.shape[0]
    first_col = fem_rank * share_cols
    slot_bank = trace_bank[:, 0]
    positions = jnp.arange(slot_total, dtype=jnp.int32)
    earlier = (slot_bank[:, None] == slot_bank[None, :]) & (positions[None, :] < positions[:, None])
    slot_place = jnp.sum(earlier.astype(jnp.int32), axis=1)
    destination = slot_bank * CAP + slot_place
    places = jnp.arange(bem_count * CAP, dtype=jnp.int32)[:, None] == destination[None, :]
    send_rows = jnp.sum(jnp.where(places, trace_row[None, :] + 1, 0), axis=1) - 1
    send_cell = jnp.sum(jnp.where(places, trace_cell[None, :] + 1, 0), axis=1) - 1
    recv_rows = lax.all_to_all(
        send_rows.reshape(bem_count, CAP), "bem", split_axis=0, concat_axis=0, tiled=True
    )
    cell_ids = jnp.arange(cell_total, dtype=jnp.int32)
    send_hot = (send_cell[:, None] == cell_ids[None, :]).astype(jnp.bfloat16)
    cell_hot = (cell_ids[:, None] == trace_cell[None, :]).astype(jnp.bfloat16)
    row_ids = jnp.arange(local_rows, dtype=jnp.int32)
    recv_hot = (recv_rows.reshape(-1)[:, None] == row_ids[None, :]).astype(jnp.bfloat16)
    node = (slot_bank * local_rows + trace_row)[:, None]
    own_first = bem_rank * local_panels
    own_centers = lax.dynamic_slice_in_dim(centers, own_first, local_panels, 0)
    offsets = own_centers[:, None, :] - centers[None, :, :]
    kernel_rows = 1.0 / (1.0 + jnp.sum(offsets * offsets, axis=-1))
    panel_ids = jnp.arange(panel_total, dtype=jnp.int32)
    own_ids = own_first + jnp.arange(local_panels, dtype=jnp.int32)
    listed = jnp.any(near_pairs[:, :, None] == panel_ids[None, None, :], axis=1)
    listed = listed | (own_ids[:, None] == panel_ids[None, :])
    kernel_rows = jnp.where(listed, 0.0, kernel_rows)
    left_wide = low_left.astype(jnp.float32)
    pair_group = lax.dynamic_slice_in_dim(near_pairs, fem_rank * group_size, group_size, 1)
    density = lax.dynamic_slice_in_dim(bem_density, first_col, share_cols, 0)
    source_part = lax.dynamic_slice_in_dim(bem_source, first_col, share_cols, 0)
    diag_row = bem_diagonal[None, :]
    fem_state = fem_field
    for sweep in range(ITERS):
        whole = bem_density if sweep == 0 else density
        narrow = whole.astype(jnp.bfloat16).reshape(-1, local_panels, panel_rows)
        narrow = jnp.transpose(narrow, (1, 0, 2))
        if sweep > 0:
            narrow = lax.all_gather(narrow, "fem", axis=1, tiled=True)
        x = lax.all_gather(narrow, "bem", axis=0, tiled=True)
        before_x, after_x = faces(fem_state, "fem", 0)
        before_y, after_y = faces(fem_state, "bem", 1)
        outgoing = jnp.dot(
            send_hot,
            fem_state.astype(jnp.bfloat16).reshape(cell_total, excitations),
            preferred_element_type=jnp.float32,
        ).astype(jnp.bfloat16)
        incoming = lax.all_to_all(
            outgoing.reshape(bem_count, CAP, excitations),
            "bem",
            split_axis=0,
            concat_axis=0,
            tiled=True,
        )
        traced = lax.dot_general(
            incoming.reshape(-1, excitations),
            recv_hot,
            (((0,), (0,)), ((), ())),
            preferred_element_type=jnp.float32,
        )
        partial_sum = near_apply(pair_group, x, near_blocks, traced)
        parts = lax.all_to_all(
            partial_sum.reshape(fem_count, share_cols, local_rows),
            "fem",
            split_axis=0,
            concat_axis=0,
            tiled=True,
        )
        own_cols = lax.dynamic_slice_in_dim(x, first_col, share_cols, 1)
        reduced = jnp.einsum(
            "qen,qrn->qer", own_cols, low_right, preferred_element_type=jnp.float32
        ).astype(jnp.bfloat16)
        reduced = lax.optimization_barrier(reduced).astype(jnp.float32)
        weights = jnp.einsum("pq,qer->per", kernel_rows, reduced, precision=HIGHEST)
        distant = jnp.einsum("per,prn->epn", weights, left_wide, precision=HIGHEST).reshape(
            share_cols, local_rows
        )
        values = pick_nodes(node, x)
        coupled = jnp.dot(cell_hot, values, preferred_element_type=jnp.float32).reshape(
            fem_state.shape
        )
        scale = (6.0 + reaction)[..., None]
        beside = neighbour_sum(fem_state, before_x, after_x, before_y, after_y)
        fem_next = fem_state + (fem_source - (scale * fem_state - beside) - coupled) / scale
        applied = distant + jnp.sum(parts.astype(jnp.float32), axis=0)
        density = density + (source_part - applied) / diag_row
        fem_state = fem_next
    return (fem_state, density)


def solution(mesh):
    return jax.shard_map(
        shards,
        mesh=mesh,
        in_specs=(
            P("fem", "bem", None, None),
            P("fem", "bem", None, None),
            P("fem", "bem", None),
            P(None, "bem"),
            P(None, "bem"),
            P("bem"),
            P("bem", "fem", None, None),
            P("bem", None),
            P("bem", None, None),
            P(),
            P(),
            P(("fem", "bem")),
            P(("fem", "bem"), None),
            P(("fem", "bem")),
        ),
        out_specs=(P("fem", "bem", None, None), P("fem", "bem")),
        check_vma=False,
    )
```

profile of v0, /device:TPU:3, one launch (start us, length us, event | category | flops | bytes accessed | tf_op | source)
XLA Modules:
  0.0 223.2 jit_solution(14401168772540910)
XLA Ops:
  7.3 1.3 copy.66
  8.6 0.9 copy.67
  9.5 0.9 convert_reduce_fusion.3
  10.4 1.2 multiply_add_fusion
  11.8 0.7 sub.67
  12.5 5.5 %all-to-all-start.1 = ((s32[8,1,32]{2,1,0:T(1,128)}), s32[8,1,32]{2,1,0:T(1,128)S(1)}, u32[]{:S(2)}, u32[]{:S(2)}) async-start(s32[8,1,32]{2,1,0:T(1,128)} %sub.67), calls=%async_computation.1 | async-start | bytes 8192 | tf_op jit(solution)/shard_map/all_to_all | solution.py:145
  18.2 0.7 fusion.64
  18.9 1.1 fusion.6
  20.1 2.9 %all-to-all-done.1 = s32[8,1,32]{2,1,0:T(1,128)S(1)} async-done(((s32[8,1,32]{2,1,0:T(1,128)}), s32[8,1,32]{2,1,0:T(1,128)S(1)}, u32[]{:S(2)}, u32[]{:S(2)}) %all-to-all-start.1) | async-done | bytes 1056 | tf_op jit(solution)/shard_map/all_to_all | solution.py:145
  23.0 3.9 %all-to-all-start = ((bf16[8,32,128]{2,1,0:T(8,128)(2,1)}), bf16[8,32,128]{2,1,0:T(8,128)(2,1)S(1)}, u32[]{:S(2)}, u32[]{:S(2)}) async-start(bf16[8,32,128]{2,1,0:T(8,128)(2,1)} %bitcast.8), calls=%async_computation | async-start | bytes 131072 | tf_op jit(solution)/shard_map/all_to_all | solution.py:183
  28.9 5.0 %all-to-all-done = bf16[8,32,128]{2,1,0:T(8,128)(2,1)S(1)} async-done(((bf16[8,32,128]{2,1,0:T(8,128)(2,1)}), bf16[8,32,128]{2,1,0:T(8,128)(2,1)S(1)}, u32[]{:S(2)}, u32[]{:S(2)}) %all-to-all-start) | async-done | bytes 65568 | tf_op jit(solution)/shard_map/all_to_all | solution.py:183
  34.3 8.0 %all-gather.4.cloned.1.call-done.x_ref = bf16[16,128,512]{2,1,0:T(8,128)(2,1)} async-done(((bf16[2,128,512]{2,1,0:T(8,128)(2,1)}), bf16[16,128,512]{2,1,0:T(8,128)(2,1)}) %all-gather.4.cloned.1.call-update) | async-done | bytes 2097168 | tf_op jit(solution)/shard_map/all_gather | solution.py:175
  42.3 4.6 %copy-done.1 = bf16[2,12,512,512]{3,2,1,0:T(8,128)(2,1)S(1)} copy-done((bf16[2,12,512,512]{3,2,1,0:T(8,128)(2,1)S(1)}, bf16[2,12,512,512]{3,2,1,0:T(8,128)(2,1)}, u32[]{:S(2)}) %copy-start.1) | copy-done | bytes 12582936
  46.9 1.6 copy-done.4
  48.5 7.9 %near.3 = bf16[128,1024]{1,0:T(8,128)(2,1)} custom-call(s32[2,12]{1,0:T(2,128)S(1)} %constant_dynamic-slice_fusion.pairs_ref, bf16[16,128,512]{2,1,0:T(8,128)(2,1)S(1)} %copy-done.4, bf16[2,12,512,512]{3,2,1,0:T(8,128)(2,1)S(1)} %copy-done.1, f32[128,1024]{1,0:T(8,128)S(1)} %fusion.41.init_ref), custom_call_target="tpu_custom_call" | custom-call | flops 1610612736 | bytes 12582912 | tf_op jit(solution)/shard_map/near/pallas_call | solution.py:55
  56.4 3.8 %all-to-all-start.2 = ((bf16[4,32,1024]{2,1,0:T(8,128)(2,1)}), bf16[4,32,1024]{2,1,0:T(8,128)(2,1)S(1)}, u32[]{:S(2)}, u32[]{:S(2)}) async-start(bf16[4,32,1024]{2,1,0:T(8,128)(2,1)} %bitcast.10), calls=%async_computation.2 | async-start | bytes 524288 | tf_op jit(solution)/shard_map/all_to_all | solution.py:197
  61.0 3.3 %all-to-all-done.2 = bf16[4,32,1024]{2,1,0:T(8,128)(2,1)S(1)} async-done(((bf16[4,32,1024]{2,1,0:T(8,128)(2,1)}), bf16[4,32,1024]{2,1,0:T(8,128)(2,1)S(1)}, u32[]{:S(2)}, u32[]{:S(2)}) %all-to-all-start.2) | async-done | bytes 262176 | tf_op jit(solution)/shard_map/all_to_all | solution.py:197
  64.4 1.7 fusion.76
  66.1 6.9 %all_gather.16 = bf16[2,128,512]{2,0,1:T(2,128)(2,1)S(1)} all-gather(bf16[2,32,512]{2,0,1:T(2,128)(2,1)S(1)} %bitcast.68), channel_id=1, replica_groups=mesh['fem'=4,'bem'=8] {'fem'}, dimensions={1}, use_global_device_ids=true | all-gather | bytes 327680 | tf_op jit(solution)/shard_map/all_gather | solution.py:174
  73.0 0.7 copy.72
  74.4 2.5 %collective-permute-start = (bf16[1,8,32,128]{3,2,1,0:T(8,128)(2,1)}, bf16[1,8,32,128]{3,2,1,0:T(8,128)(2,1)S(1)}, u32[]{:S(2)}, u32[]{:S(2)}) collective-permute-start(bf16[1,8,32,128]{3,2,1,0:T(8,128)(2,1)} %get-tuple-element.20), channel_id=1, source_target_pairs={{8,0},{16,8},{24,16},{9,1},{17,9},{25,17},{10,2},{18,10},{26,18},{... | collective-permute-start | bytes 196616 | tf_op jit(solution)/shard_map/ppermute | solution.py:21
  76.9 3.7 %collective-permute-start.1 = (bf16[1,8,32,128]{3,2,1,0:T(8,128)(2,1)S(1)}, bf16[1,8,32,128]{3,2,1,0:T(8,128)(2,1)S(1)}, u32[]{:S(2)}, u32[]{:S(2)}) collective-permute-start(bf16[1,8,32,128]{3,2,1,0:T(8,128)(2,1)S(1)} %get-tuple-element.21), channel_id=1, source_target_pairs={{0,8},{8,16},{16,24},{1,9},{9,17},{17,25},{2,10},{10,18},{18,26},{... | collective-permute-start | bytes 196616 | tf_op jit(solution)/shard_map/ppermute | solution.py:21
  81.2 5.5 %collective-permute-start.2 = (bf16[8,1,32,128]{3,2,1,0:T(8,128)(2,1)}, bf16[8,1,32,128]{3,2,1,0:T(8,128)(2,1)S(1)}, u32[]{:S(2)}, u32[]{:S(2)}) collective-permute-start(bf16[8,1,32,128]{3,2,1,0:T(8,128)(2,1)} %get-tuple-element.22), channel_id=1, source_target_pairs={{1,0},{2,1},{3,2},{4,3},{5,4},{6,5},{7,6},{9,8},{10,9},{11,10},{12... | collective-permute-start | bytes 196616 | tf_op jit(solution)/shard_map/ppermute | solution.py:21
  86.7 2.2 collective-permute-start.3
  88.9 0.8 broadcast_add_fusion
  89.7 0.7 copy.68.node_ref
  90.5 2.2 collective-permute-done.2
  92.7 4.4 %pick.3 = bf16[256,128]{1,0:T(8,128)(2,1)S(1)} custom-call(s32[256,1]{1,0:T(8,128)S(1)} %copy.68.node_ref, bf16[16,128,512]{2,1,0:T(8,128)(2,1)S(1)} %copy-done.5), custom_call_target="tpu_custom_call" | custom-call | flops 536870912 | bytes 2097152 | tf_op jit(solution)/shard_map/pick/pallas_call | solution.py:97
  97.6 2.1 fusion.74
  100.2 10.2 %all_to_all.36 = bf16[8,32,128]{2,1,0:T(8,128)(2,1)S(1)} all-to-all(bf16[8,32,128]{2,1,0:T(8,128)(2,1)S(1)} %bitcast.71), channel_id=1, replica_groups=mesh['fem'=4,'bem'=8] {'bem'}, dimensions={0} | all-to-all | bytes 131072 | tf_op jit(solution)/shard_map/all_to_all | solution.py:183
  110.9 4.6 %copy-done.2 = bf16[2,12,512,512]{3,2,1,0:T(8,128)(2,1)S(1)} copy-done((bf16[2,12,512,512]{3,2,1,0:T(8,128)(2,1)S(1)}, bf16[2,12,512,512]{3,2,1,0:T(8,128)(2,1)}, u32[]{:S(2)}) %copy-start.2) | copy-done | bytes 12582936
  115.4 1.6 copy-done.6
  117.0 7.9 %near.4 = bf16[128,1024]{1,0:T(8,128)(2,1)} custom-call(s32[2,12]{1,0:T(2,128)S(1)} %constant_dynamic-slice_fusion.pairs_ref, bf16[16,128,512]{2,1,0:T(8,128)(2,1)S(1)} %copy-done.6, bf16[2,12,512,512]{3,2,1,0:T(8,128)(2,1)S(1)} %copy-done.2, f32[128,1024]{1,0:T(8,128)S(1)} %fusion.40.init_ref), custom_call_target="tpu_custom_call" | custom-call | flops 1610612736 | bytes 12582912 | tf_op jit(solution)/shard_map/near/pallas_call | solution.py:55
  125.0 4.1 %all-to-all-start.4 = ((bf16[4,32,1024]{2,1,0:T(8,128)(2,1)}), bf16[4,32,1024]{2,1,0:T(8,128)(2,1)S(1)}, u32[]{:S(2)}, u32[]{:S(2)}) async-start(bf16[4,32,1024]{2,1,0:T(8,128)(2,1)} %bitcast.17), calls=%async_computation.4 | async-start | bytes 524288 | tf_op jit(solution)/shard_map/all_to_all | solution.py:197
  129.4 0.9 fusion.57
  130.4 1.0 convolution_bitcast_fusion.1
  131.4 0.7 copy.83
  132.0 0.9 all-to-all-done.4
  133.0 1.7 fusion.73
  134.8 6.7 %all_gather.18 = bf16[2,128,512]{2,0,1:T(2,128)(2,1)S(1)} all-gather(bf16[2,32,512]{2,0,1:T(2,128)(2,1)S(1)} %bitcast.70), channel_id=1, replica_groups=mesh['fem'=4,'bem'=8] {'fem'}, dimensions={1}, use_global_device_ids=true | all-gather | bytes 327680 | tf_op jit(solution)/shard_map/all_gather | solution.py:174
  141.5 0.7 copy.77
  142.3 2.9 %collective-permute-start.4 = (bf16[1,8,32,128]{3,2,1,0:T(8,128)(2,1)S(1)}, bf16[1,8,32,128]{3,2,1,0:T(8,128)(2,1)S(1)}, u32[]{:S(2)}, u32[]{:S(2)}) collective-permute-start(bf16[1,8,32,128]{3,2,1,0:T(8,128)(2,1)S(1)} %get-tuple-element.16), channel_id=1, source_target_pairs={{8,0},{16,8},{24,16},{9,1},{17,9},{25,17},{10,2},{18,10},{26,18},{... | collective-permute-start | bytes 196616 | tf_op jit(solution)/shard_map/ppermute | solution.py:21
  145.2 3.2 %collective-permute-start.5 = (bf16[1,8,32,128]{3,2,1,0:T(8,128)(2,1)S(1)}, bf16[1,8,32,128]{3,2,1,0:T(8,128)(2,1)S(1)}, u32[]{:S(2)}, u32[]{:S(2)}) collective-permute-start(bf16[1,8,32,128]{3,2,1,0:T(8,128)(2,1)S(1)} %get-tuple-element.17), channel_id=1, source_target_pairs={{0,8},{8,16},{16,24},{1,9},{9,17},{17,25},{2,10},{10,18},{18,26},{... | collective-permute-start | bytes 196616 | tf_op jit(solution)/shard_map/ppermute | solution.py:21
  148.5 6.3 %collective-permute-start.6 = (bf16[8,1,32,128]{3,2,1,0:T(8,128)(2,1)S(1)}, bf16[8,1,32,128]{3,2,1,0:T(8,128)(2,1)S(1)}, u32[]{:S(2)}, u32[]{:S(2)}) collective-permute-start(bf16[8,1,32,128]{3,2,1,0:T(8,128)(2,1)S(1)} %get-tuple-element.18), channel_id=1, source_target_pairs={{1,0},{2,1},{3,2},{4,3},{5,4},{6,5},{7,6},{9,8},{10,9},{11,10},{12... | collective-permute-start | bytes 196616 | tf_op jit(solution)/shard_map/ppermute | solution.py:21
  154.8 2.4 %collective-permute-start.7 = (bf16[8,1,32,128]{3,2,1,0:T(8,128)(2,1)S(1)}, bf16[8,1,32,128]{3,2,1,0:T(8,128)(2,1)S(1)}, u32[]{:S(2)}, u32[]{:S(2)}) collective-permute-start(bf16[8,1,32,128]{3,2,1,0:T(8,128)(2,1)S(1)} %get-tuple-element.19), channel_id=1, source_target_pairs={{0,1},{1,2},{2,3},{3,4},{4,5},{5,6},{6,7},{8,9},{9,10},{10,11},{11... | collective-permute-start | bytes 196616 | tf_op jit(solution)/shard_map/ppermute | solution.py:21
  157.2 3.2 %collective-permute-done.6 = bf16[8,1,32,128]{3,2,1,0:T(8,128)(2,1)S(1)} collective-permute-done((bf16[8,1,32,128]{3,2,1,0:T(8,128)(2,1)S(1)}, bf16[8,1,32,128]{3,2,1,0:T(8,128)(2,1)S(1)}, u32[]{:S(2)}, u32[]{:S(2)}) %collective-permute-start.6) | collective-permute-done | bytes 65568 | tf_op jit(solution)/shard_map/ppermute | solution.py:21
  160.5 4.4 %pick.4 = bf16[256,128]{1,0:T(8,128)(2,1)S(1)} custom-call(s32[256,1]{1,0:T(8,128)S(1)} %copy.68.node_ref, bf16[16,128,512]{2,1,0:T(8,128)(2,1)S(1)} %copy-done.7), custom_call_target="tpu_custom_call" | custom-call | flops 536870912 | bytes 2097152 | tf_op jit(solution)/shard_map/pick/pallas_call | solution.py:97
  165.4 2.1 fusion.71
  167.5 1.1 fusion.8
  168.6 5.4 %all-to-all-start.5 = ((bf16[8,32,128]{2,1,0:T(8,128)(2,1)}), bf16[8,32,128]{2,1,0:T(8,128)(2,1)S(1)}, u32[]{:S(2)}, u32[]{:S(2)}) async-start(bf16[8,32,128]{2,1,0:T(8,128)(2,1)} %bitcast.22), calls=%async_computation.5 | async-start | bytes 131072 | tf_op jit(solution)/shard_map/all_to_all | solution.py:183
  174.1 2.2 %collective-permute-start.8 = (bf16[1,8,32,128]{3,2,1,0:T(8,128)(2,1)S(1)}, bf16[1,8,32,128]{3,2,1,0:T(8,128)(2,1)S(1)}, u32[]{:S(2)}, u32[]{:S(2)}) collective-permute-start(bf16[1,8,32,128]{3,2,1,0:T(8,128)(2,1)S(1)} %get-tuple-element.12), channel_id=1, source_target_pairs={{8,0},{16,8},{24,16},{9,1},{17,9},{25,17},{10,2},{18,10},{26,18},{... | collective-permute-start | bytes 196616 | tf_op jit(solution)/shard_map/ppermute | solution.py:21
  176.3 3.9 %collective-permute-start.9 = (bf16[1,8,32,128]{3,2,1,0:T(8,128)(2,1)S(1)}, bf16[1,8,32,128]{3,2,1,0:T(8,128)(2,1)S(1)}, u32[]{:S(2)}, u32[]{:S(2)}) collective-permute-start(bf16[1,8,32,128]{3,2,1,0:T(8,128)(2,1)S(1)} %get-tuple-element.13), channel_id=1, source_target_pairs={{0,8},{8,16},{16,24},{1,9},{9,17},{17,25},{2,10},{10,18},{18,26},{... | collective-permute-start | bytes 196616 | tf_op jit(solution)/shard_map/ppermute | solution.py:21
  180.3 2.5 %collective-permute-start.10 = (bf16[8,1,32,128]{3,2,1,0:T(8,128)(2,1)S(1)}, bf16[8,1,32,128]{3,2,1,0:T(8,128)(2,1)S(1)}, u32[]{:S(2)}, u32[]{:S(2)}) collective-permute-start(bf16[8,1,32,128]{3,2,1,0:T(8,128)(2,1)S(1)} %get-tuple-element.14), channel_id=1, source_target_pairs={{1,0},{2,1},{3,2},{4,3},{5,4},{6,5},{7,6},{9,8},{10,9},{11,10},{12... | collective-permute-start | bytes 196616 | tf_op jit(solution)/shard_map/ppermute | solution.py:21
  182.7 3.5 %collective-permute-start.11 = (bf16[8,1,32,128]{3,2,1,0:T(8,128)(2,1)S(1)}, bf16[8,1,32,128]{3,2,1,0:T(8,128)(2,1)S(1)}, u32[]{:S(2)}, u32[]{:S(2)}) collective-permute-start(bf16[8,1,32,128]{3,2,1,0:T(8,128)(2,1)S(1)} %get-tuple-element.15), channel_id=1, source_target_pairs={{0,1},{1,2},{2,3},{3,4},{4,5},{5,6},{6,7},{8,9},{9,10},{10,11},{11... | collective-permute-start | bytes 196616 | tf_op jit(solution)/shard_map/ppermute | solution.py:21
  186.3 0.7 convert_element_type.115
  187.6 0.7 convert_element_type.117
  188.3 0.7 convert_element_type.118
  189.4 4.6 %copy-done.3 = bf16[2,12,512,512]{3,2,1,0:T(8,128)(2,1)S(1)} copy-done((bf16[2,12,512,512]{3,2,1,0:T(8,128)(2,1)S(1)}, bf16[2,12,512,512]{3,2,1,0:T(8,128)(2,1)}, u32[]{:S(2)}) %copy-start.3) | copy-done | bytes 12582936
  194.0 1.6 copy-done.8
  195.6 7.9 %near.5 = bf16[128,1024]{1,0:T(8,128)(2,1)} custom-call(s32[2,12]{1,0:T(2,128)S(1)} %constant_dynamic-slice_fusion.pairs_ref, bf16[16,128,512]{2,1,0:T(8,128)(2,1)S(1)} %copy-done.8, bf16[2,12,512,512]{3,2,1,0:T(8,128)(2,1)S(1)} %copy-done.3, f32[128,1024]{1,0:T(8,128)S(1)} %fusion.39.init_ref), custom_call_target="tpu_custom_call" | custom-call | flops 1610612736 | bytes 12582912 | tf_op jit(solution)/shard_map/near/pallas_call | solution.py:55
  203.5 3.4 %all-to-all-start.6 = ((bf16[4,32,1024]{2,1,0:T(8,128)(2,1)}), bf16[4,32,1024]{2,1,0:T(8,128)(2,1)S(1)}, u32[]{:S(2)}, u32[]{:S(2)}) async-start(bf16[4,32,1024]{2,1,0:T(8,128)(2,1)} %bitcast.24), calls=%async_computation.6 | async-start | bytes 524288 | tf_op jit(solution)/shard_map/all_to_all | solution.py:197
  207.3 4.4 %pick.5 = bf16[256,128]{1,0:T(8,128)(2,1)S(1)} custom-call(s32[256,1]{1,0:T(8,128)S(1)} %copy.68.node_ref, bf16[16,128,512]{2,1,0:T(8,128)(2,1)S(1)} %copy-done.9), custom_call_target="tpu_custom_call" | custom-call | flops 536870912 | bytes 2097152 | tf_op jit(solution)/shard_map/pick/pallas_call | solution.py:97
  212.3 2.2 fusion.29
  215.0 1.6 divide_add_fusion
  (149 shorter events, 9.6 us)
Async XLA Ops:
  7.2 53.0 %copy-start = (bf16[16,32,512]{2,1,0:T(8,128)(2,1)S(1)}, bf16[16,32,512]{2,1,0:T(8,128)(2,1)}, u32[]{:S(2)}) copy-start(bf16[16,32,512]{2,1,0:T(8,128)(2,1)} %param.23) | copy-start | bytes 1572868
  7.2 10.9 %copy-start.14 = (f32[8,8,32,128]{3,2,1,0:T(8,128)S(1)}, f32[8,8,32,128]{3,2,1,0:T(8,128)}, u32[]{:S(2)}) copy-start(f32[8,8,32,128]{3,2,1,0:T(8,128)} %param.14) | copy-start | bytes 3145732
  7.2 11.0 %copy-start.35 = (f32[16,3]{0,1:T(4,128)S(1)}, f32[16,3]{0,1:T(4,128)}, u32[]{:S(2)}) copy-start(f32[16,3]{0,1:T(4,128)} %param.24) | copy-start | bytes 580
  7.2 11.0 %copy-start.40 = (s32[2,48]{1,0:T(2,128)S(1)}, s32[2,48]{1,0:T(2,128)}, u32[]{:S(2)}) copy-start(s32[2,48]{1,0:T(2,128)} %param.21) | copy-start | bytes 1156
  7.2 35.1 %all-gather.4.cloned.1.call-start = ((), (), s32[]{:S(2)}) async-start(), calls=%async_computation.7 | async-start | bytes 2359296 | tf_op jit(solution)/shard_map/all_gather | solution.py:175
  12.5 10.5 %all-to-all-start.1 = ((s32[8,1,32]{2,1,0:T(1,128)}), s32[8,1,32]{2,1,0:T(1,128)S(1)}, u32[]{:S(2)}, u32[]{:S(2)}) async-start(s32[8,1,32]{2,1,0:T(1,128)} %sub.67), calls=%async_computation.1 | async-start | bytes 8192 | tf_op jit(solution)/shard_map/all_to_all | solution.py:145
  18.1 16.2 %copy-start.17 = (bf16[8,8,32,128]{3,2,1,0:T(8,128)(2,1)}, bf16[8,8,32,128]{3,2,1,0:T(8,128)(2,1)S(1)}, u32[]{:S(2)}) copy-start(bf16[8,8,32,128]{3,2,1,0:T(8,128)(2,1)S(1)} %convert.18) | copy-start | bytes 1572868
  18.9 4.1 %copy-start.41 = (s32[256]{0:T(256)}, s32[256]{0:T(256)S(1)}, u32[]{:S(2)}) copy-start(s32[256]{0:T(256)S(1)} %broadcast_add_fusion.2) | copy-start | bytes 3076
  23.0 10.9 %all-to-all-start = ((bf16[8,32,128]{2,1,0:T(8,128)(2,1)}), bf16[8,32,128]{2,1,0:T(8,128)(2,1)S(1)}, u32[]{:S(2)}, u32[]{:S(2)}) async-start(bf16[8,32,128]{2,1,0:T(8,128)(2,1)} %bitcast.8), calls=%async_computation | async-start | bytes 131072 | tf_op jit(solution)/shard_map/all_to_all | solution.py:183
  27.6 32.9 %copy-start.33 = (f32[2,16]{1,0:T(2,128)}, f32[2,16]{1,0:T(2,128)S(1)}, u32[]{:S(2)}) copy-start(f32[2,16]{1,0:T(2,128)S(1)} %multiply_reduce_fusion) | copy-start | bytes 388
  42.3 4.6 %copy-start.1 = (bf16[2,12,512,512]{3,2,1,0:T(8,128)(2,1)S(1)}, bf16[2,12,512,512]{3,2,1,0:T(8,128)(2,1)}, u32[]{:S(2)}) copy-start(bf16[2,12,512,512]{3,2,1,0:T(8,128)(2,1)} %blocks_ref.5) | copy-start | bytes 37748740
  46.9 1.6 copy-start.4
  48.5 11.7 %copy-start.5 = (bf16[16,128,512]{2,1,0:T(8,128)(2,1)S(1)}, bf16[16,128,512]{2,1,0:T(8,128)(2,1)}, u32[]{:S(2)}) copy-start(bf16[16,128,512]{2,1,0:T(8,128)(2,1)} %all-gather.4.cloned.1.call-done.x_ref) | copy-start | bytes 6291460
  48.5 12.0 %copy-start.36 = (pred[2,16]{1,0:T(4,128)(4,1)S(1)}, pred[2,16]{1,0:T(4,128)(4,1)}, u32[]{:S(2)}) copy-start(pred[2,16]{1,0:T(4,128)(4,1)} %fusion.64) | copy-start | bytes 100
  48.5 12.0 %copy-start.38 = (s32[2]{0:T(128)S(1)}, s32[2]{0:T(128)}, u32[]{:S(2)}) copy-start(s32[2]{0:T(128)} %iota_add_fusion) | copy-start | bytes 28
  48.5 12.3 %copy-start.21 = (bf16[2,32,512]{2,1,0:T(8,128)(2,1)S(1)}, bf16[2,32,512]{2,1,0:T(8,128)(2,1)}, u32[]{:S(2)}) copy-start(bf16[2,32,512]{2,1,0:T(8,128)(2,1)} %param.22) | copy-start | bytes 196612
  56.4 8.0 %copy-start.31 = (f32[1024]{0:T(1024)S(1)}, f32[1024]{0:T(1024)}, u32[]{:S(2)}) copy-start(f32[1024]{0:T(1024)} %param.19) | copy-start | bytes 12292
  56.4 7.9 %all-to-all-start.2 = ((bf16[4,32,1024]{2,1,0:T(8,128)(2,1)}), bf16[4,32,1024]{2,1,0:T(8,128)(2,1)S(1)}, u32[]{:S(2)}, u32[]{:S(2)}) async-start(bf16[4,32,1024]{2,1,0:T(8,128)(2,1)} %bitcast.10), calls=%async_computation.2 | async-start | bytes 524288 | tf_op jit(solution)/shard_map/all_to_all | solution.py:197
  60.2 13.6 %copy-start.18 = (bf16[8,8,32,128]{3,2,1,0:T(8,128)(2,1)S(1)}, bf16[8,8,32,128]{3,2,1,0:T(8,128)(2,1)}, u32[]{:S(2)}) copy-start(bf16[8,8,32,128]{3,2,1,0:T(8,128)(2,1)} %copy-done.17) | copy-start | bytes 1572868
  60.2 50.7 %all-gather.6.cloned.1.call-start = ((), (), s32[]{:S(2)}) async-start(), calls=%async_computation.8 | async-start | bytes 2359296 | tf_op jit(solution)/shard_map/all_gather | solution.py:175
  73.7 23.4 %copy-start.32 = (s32[256]{0:T(256)S(1)}, s32[256]{0:T(256)}, u32[]{:S(2)}) copy-start(s32[256]{0:T(256)} %param.25) | copy-start | bytes 3076
  74.4 16.1 %collective-permute-start = (bf16[1,8,32,128]{3,2,1,0:T(8,128)(2,1)}, bf16[1,8,32,128]{3,2,1,0:T(8,128)(2,1)S(1)}, u32[]{:S(2)}, u32[]{:S(2)}) collective-permute-start(bf16[1,8,32,128]{3,2,1,0:T(8,128)(2,1)} %get-tuple-element.20), channel_id=1, source_target_pairs={{8,0},{16,8},{24,16},{9,1},{17,9},{25,17},{10,2},{18,10},{26,18},{... | collective-permute-start | bytes 196616 | tf_op jit(solution)/shard_map/ppermute | solution.py:21
  76.9 13.6 %collective-permute-start.1 = (bf16[1,8,32,128]{3,2,1,0:T(8,128)(2,1)S(1)}, bf16[1,8,32,128]{3,2,1,0:T(8,128)(2,1)S(1)}, u32[]{:S(2)}, u32[]{:S(2)}) collective-permute-start(bf16[1,8,32,128]{3,2,1,0:T(8,128)(2,1)S(1)} %get-tuple-element.21), channel_id=1, source_target_pairs={{0,8},{8,16},{16,24},{1,9},{9,17},{17,25},{2,10},{10,18},{18,26},{... | collective-permute-start | bytes 196616 | tf_op jit(solution)/shard_map/ppermute | solution.py:21
  81.2 11.5 %collective-permute-start.2 = (bf16[8,1,32,128]{3,2,1,0:T(8,128)(2,1)}, bf16[8,1,32,128]{3,2,1,0:T(8,128)(2,1)S(1)}, u32[]{:S(2)}, u32[]{:S(2)}) collective-permute-start(bf16[8,1,32,128]{3,2,1,0:T(8,128)(2,1)} %get-tuple-element.22), channel_id=1, source_target_pairs={{1,0},{2,1},{3,2},{4,3},{5,4},{6,5},{7,6},{9,8},{10,9},{11,10},{12... | collective-permute-start | bytes 196616 | tf_op jit(solution)/shard_map/ppermute | solution.py:21
  86.7 6.0 %collective-permute-start.3 = (bf16[8,1,32,128]{3,2,1,0:T(8,128)(2,1)S(1)}, bf16[8,1,32,128]{3,2,1,0:T(8,128)(2,1)S(1)}, u32[]{:S(2)}, u32[]{:S(2)}) collective-permute-start(bf16[8,1,32,128]{3,2,1,0:T(8,128)(2,1)S(1)} %get-tuple-element.23), channel_id=1, source_target_pairs={{0,1},{1,2},{2,3},{3,4},{4,5},{5,6},{6,7},{8,9},{9,10},{10,11},{11... | collective-permute-start | bytes 196616 | tf_op jit(solution)/shard_map/ppermute | solution.py:21
  89.7 7.9 %copy-start.23 = (f32[8,8,32]{2,1,0:T(8,128)}, f32[8,8,32]{2,1,0:T(8,128)S(1)}, u32[]{:S(2)}) copy-start(f32[8,8,32]{2,1,0:T(8,128)S(1)} %broadcast_add_fusion) | copy-start | bytes 24580
  90.4 7.2 %copy-start.10 = (f32[8,8,32,128]{3,2,1,0:T(8,128)S(1)}, f32[8,8,32,128]{3,2,1,0:T(8,128)}, u32[]{:S(2)}) copy-start(f32[8,8,32,128]{3,2,1,0:T(8,128)} %param.15) | copy-start | bytes 3145732
  90.4 7.2 %copy-start.15 = (f32[8,8,32,128]{3,2,1,0:T(8,128)S(1)}, f32[8,8,32,128]{3,2,1,0:T(8,128)}, u32[]{:S(2)}) copy-start(f32[8,8,32,128]{3,2,1,0:T(8,128)} %param.14) | copy-start | bytes 3145732
  97.6 2.1 copy-start.42
  99.7 10.7 %copy-start.19 = (bf16[8,8,32,128]{3,2,1,0:T(8,128)(2,1)}, bf16[8,8,32,128]{3,2,1,0:T(8,128)(2,1)S(1)}, u32[]{:S(2)}) copy-start(bf16[8,8,32,128]{3,2,1,0:T(8,128)(2,1)S(1)} %get-tuple-element.8) | copy-start | bytes 1572868
  110.9 4.6 %copy-start.2 = (bf16[2,12,512,512]{3,2,1,0:T(8,128)(2,1)S(1)}, bf16[2,12,512,512]{3,2,1,0:T(8,128)(2,1)}, u32[]{:S(2)}) copy-start(bf16[2,12,512,512]{3,2,1,0:T(8,128)(2,1)} %blocks_ref.5) | copy-start | bytes 37748740
  117.0 12.1 %copy-start.7 = (bf16[16,128,512]{2,1,0:T(8,128)(2,1)S(1)}, bf16[16,128,512]{2,1,0:T(8,128)(2,1)}, u32[]{:S(2)}) copy-start(bf16[16,128,512]{2,1,0:T(8,128)(2,1)} %all-gather.6.cloned.1.call-done.x_ref) | copy-start | bytes 6291460
  125.0 8.0 %all-to-all-start.4 = ((bf16[4,32,1024]{2,1,0:T(8,128)(2,1)}), bf16[4,32,1024]{2,1,0:T(8,128)(2,1)S(1)}, u32[]{:S(2)}, u32[]{:S(2)}) async-start(bf16[4,32,1024]{2,1,0:T(8,128)(2,1)} %bitcast.17), calls=%async_computation.4 | async-start | bytes 524288 | tf_op jit(solution)/shard_map/all_to_all | solution.py:197
  129.1 13.1 %copy-start.20 = (bf16[8,8,32,128]{3,2,1,0:T(8,128)(2,1)S(1)}, bf16[8,8,32,128]{3,2,1,0:T(8,128)(2,1)}, u32[]{:S(2)}) copy-start(bf16[8,8,32,128]{3,2,1,0:T(8,128)(2,1)} %copy-done.19) | copy-start | bytes 1572868
  129.1 60.3 %all-gather.8.cloned.1.call-start = ((), (), s32[]{:S(2)}) async-start(), calls=%async_computation.9 | async-start | bytes 2359296 | tf_op jit(solution)/shard_map/all_gather | solution.py:175
  142.3 14.9 %collective-permute-start.4 = (bf16[1,8,32,128]{3,2,1,0:T(8,128)(2,1)S(1)}, bf16[1,8,32,128]{3,2,1,0:T(8,128)(2,1)S(1)}, u32[]{:S(2)}, u32[]{:S(2)}) collective-permute-start(bf16[1,8,32,128]{3,2,1,0:T(8,128)(2,1)S(1)} %get-tuple-element.16), channel_id=1, source_target_pairs={{8,0},{16,8},{24,16},{9,1},{17,9},{25,17},{10,2},{18,10},{26,18},{... | collective-permute-start | bytes 196616 | tf_op jit(solution)/shard_map/ppermute | solution.py:21
  145.2 12.0 %collective-permute-start.5 = (bf16[1,8,32,128]{3,2,1,0:T(8,128)(2,1)S(1)}, bf16[1,8,32,128]{3,2,1,0:T(8,128)(2,1)S(1)}, u32[]{:S(2)}, u32[]{:S(2)}) collective-permute-start(bf16[1,8,32,128]{3,2,1,0:T(8,128)(2,1)S(1)} %get-tuple-element.17), channel_id=1, source_target_pairs={{0,8},{8,16},{16,24},{1,9},{9,17},{17,25},{2,10},{10,18},{18,26},{... | collective-permute-start | bytes 196616 | tf_op jit(solution)/shard_map/ppermute | solution.py:21
  148.5 12.0 %collective-permute-start.6 = (bf16[8,1,32,128]{3,2,1,0:T(8,128)(2,1)S(1)}, bf16[8,1,32,128]{3,2,1,0:T(8,128)(2,1)S(1)}, u32[]{:S(2)}, u32[]{:S(2)}) collective-permute-start(bf16[8,1,32,128]{3,2,1,0:T(8,128)(2,1)S(1)} %get-tuple-element.18), channel_id=1, source_target_pairs={{1,0},{2,1},{3,2},{4,3},{5,4},{6,5},{7,6},{9,8},{10,9},{11,10},{12... | collective-permute-start | bytes 196616 | tf_op jit(solution)/shard_map/ppermute | solution.py:21
  154.7 10.6 %copy-start.11 = (f32[8,8,32,128]{3,2,1,0:T(8,128)S(1)}, f32[8,8,32,128]{3,2,1,0:T(8,128)}, u32[]{:S(2)}) copy-start(f32[8,8,32,128]{3,2,1,0:T(8,128)} %param.15) | copy-start | bytes 3145732
  154.7 10.6 %copy-start.13 = (f32[8,8,32,128]{3,2,1,0:T(8,128)S(1)}, f32[8,8,32,128]{3,2,1,0:T(8,128)}, u32[]{:S(2)}) copy-start(f32[8,8,32,128]{3,2,1,0:T(8,128)} %get-tuple-element.9) | copy-start | bytes 3145732
  154.7 10.6 %copy-start.24 = (f32[8,8,32]{2,1,0:T(8,128)S(1)}, f32[8,8,32]{2,1,0:T(8,128)}, u32[]{:S(2)}) copy-start(f32[8,8,32]{2,1,0:T(8,128)} %copy-done.23) | copy-start | bytes 24580
  154.8 5.7 %collective-permute-start.7 = (bf16[8,1,32,128]{3,2,1,0:T(8,128)(2,1)S(1)}, bf16[8,1,32,128]{3,2,1,0:T(8,128)(2,1)S(1)}, u32[]{:S(2)}, u32[]{:S(2)}) collective-permute-start(bf16[8,1,32,128]{3,2,1,0:T(8,128)(2,1)S(1)} %get-tuple-element.19), channel_id=1, source_target_pairs={{0,1},{1,2},{2,3},{3,4},{4,5},{5,6},{6,7},{8,9},{9,10},{10,11},{11... | collective-permute-start | bytes 196616 | tf_op jit(solution)/shard_map/ppermute | solution.py:21
  165.4 2.1 copy-start.43
  168.6 20.3 %all-to-all-start.5 = ((bf16[8,32,128]{2,1,0:T(8,128)(2,1)}), bf16[8,32,128]{2,1,0:T(8,128)(2,1)S(1)}, u32[]{:S(2)}, u32[]{:S(2)}) async-start(bf16[8,32,128]{2,1,0:T(8,128)(2,1)} %bitcast.22), calls=%async_computation.5 | async-start | bytes 131072 | tf_op jit(solution)/shard_map/all_to_all | solution.py:183
  174.1 12.2 %collective-permute-start.8 = (bf16[1,8,32,128]{3,2,1,0:T(8,128)(2,1)S(1)}, bf16[1,8,32,128]{3,2,1,0:T(8,128)(2,1)S(1)}, u32[]{:S(2)}, u32[]{:S(2)}) collective-permute-start(bf16[1,8,32,128]{3,2,1,0:T(8,128)(2,1)S(1)} %get-tuple-element.12), channel_id=1, source_target_pairs={{8,0},{16,8},{24,16},{9,1},{17,9},{25,17},{10,2},{18,10},{26,18},{... | collective-permute-start | bytes 196616 | tf_op jit(solution)/shard_map/ppermute | solution.py:21
  176.3 10.7 %collective-permute-start.9 = (bf16[1,8,32,128]{3,2,1,0:T(8,128)(2,1)S(1)}, bf16[1,8,32,128]{3,2,1,0:T(8,128)(2,1)S(1)}, u32[]{:S(2)}, u32[]{:S(2)}) collective-permute-start(bf16[1,8,32,128]{3,2,1,0:T(8,128)(2,1)S(1)} %get-tuple-element.13), channel_id=1, source_target_pairs={{0,8},{8,16},{16,24},{1,9},{9,17},{17,25},{2,10},{10,18},{18,26},{... | collective-permute-start | bytes 196616 | tf_op jit(solution)/shard_map/ppermute | solution.py:21
  180.3 7.4 %collective-permute-start.10 = (bf16[8,1,32,128]{3,2,1,0:T(8,128)(2,1)S(1)}, bf16[8,1,32,128]{3,2,1,0:T(8,128)(2,1)S(1)}, u32[]{:S(2)}, u32[]{:S(2)}) collective-permute-start(bf16[8,1,32,128]{3,2,1,0:T(8,128)(2,1)S(1)} %get-tuple-element.14), channel_id=1, source_target_pairs={{1,0},{2,1},{3,2},{4,3},{5,4},{6,5},{7,6},{9,8},{10,9},{11,10},{12... | collective-permute-start | bytes 196616 | tf_op jit(solution)/shard_map/ppermute | solution.py:21
  182.7 5.6 %collective-permute-start.11 = (bf16[8,1,32,128]{3,2,1,0:T(8,128)(2,1)S(1)}, bf16[8,1,32,128]{3,2,1,0:T(8,128)(2,1)S(1)}, u32[]{:S(2)}, u32[]{:S(2)}) collective-permute-start(bf16[8,1,32,128]{3,2,1,0:T(8,128)(2,1)S(1)} %get-tuple-element.15), channel_id=1, source_target_pairs={{0,1},{1,2},{2,3},{3,4},{4,5},{5,6},{6,7},{8,9},{9,10},{10,11},{11... | collective-permute-start | bytes 196616 | tf_op jit(solution)/shard_map/ppermute | solution.py:21
  189.4 4.6 %copy-start.3 = (bf16[2,12,512,512]{3,2,1,0:T(8,128)(2,1)S(1)}, bf16[2,12,512,512]{3,2,1,0:T(8,128)(2,1)}, u32[]{:S(2)}) copy-start(bf16[2,12,512,512]{3,2,1,0:T(8,128)(2,1)} %blocks_ref.5) | copy-start | bytes 37748740
  194.0 1.6 copy-start.8
  195.6 11.3 %copy-start.9 = (bf16[16,128,512]{2,1,0:T(8,128)(2,1)S(1)}, bf16[16,128,512]{2,1,0:T(8,128)(2,1)}, u32[]{:S(2)}) copy-start(bf16[16,128,512]{2,1,0:T(8,128)(2,1)} %all-gather.8.cloned.1.call-done.x_ref) | copy-start | bytes 6291460
  203.5 11.5 %all-to-all-start.6 = ((bf16[4,32,1024]{2,1,0:T(8,128)(2,1)}), bf16[4,32,1024]{2,1,0:T(8,128)(2,1)S(1)}, u32[]{:S(2)}, u32[]{:S(2)}) async-start(bf16[4,32,1024]{2,1,0:T(8,128)(2,1)} %bitcast.24), calls=%async_computation.6 | async-start | bytes 524288 | tf_op jit(solution)/shard_map/all_to_all | solution.py:197
  206.9 5.2 %copy-start.12 = (f32[8,8,32,128]{3,2,1,0:T(8,128)S(1)}, f32[8,8,32,128]{3,2,1,0:T(8,128)}, u32[]{:S(2)}) copy-start(f32[8,8,32,128]{3,2,1,0:T(8,128)} %param.15) | copy-start | bytes 3145732
  206.9 5.2 %copy-start.16 = (f32[8,8,32,128]{3,2,1,0:T(8,128)S(1)}, f32[8,8,32,128]{3,2,1,0:T(8,128)}, u32[]{:S(2)}) copy-start(f32[8,8,32,128]{3,2,1,0:T(8,128)} %get-tuple-element.5) | copy-start | bytes 3145732
  206.9 5.2 %copy-start.25 = (f32[8,8,32]{2,1,0:T(8,128)S(1)}, f32[8,8,32]{2,1,0:T(8,128)}, u32[]{:S(2)}) copy-start(f32[8,8,32]{2,1,0:T(8,128)} %copy-done.23) | copy-start | bytes 24580
  207.0 5.2 %copy-start.26 = (f32[1,8,32,128]{3,2,1,0:T(8,128)S(1)}, f32[1,8,32,128]{3,2,1,0:T(8,128)}, u32[]{:S(2)}) copy-start(f32[1,8,32,128]{3,2,1,0:T(8,128)} %convert_element_type.115) | copy-start | bytes 393220
  207.0 5.2 %copy-start.27 = (f32[1,8,32,128]{3,2,1,0:T(8,128)S(1)}, f32[1,8,32,128]{3,2,1,0:T(8,128)}, u32[]{:S(2)}) copy-start(f32[1,8,32,128]{3,2,1,0:T(8,128)} %convert_element_type.116) | copy-start | bytes 393220
  207.0 5.2 %copy-start.28 = (f32[8,1,32,128]{3,2,1,0:T(8,128)S(1)}, f32[8,1,32,128]{3,2,1,0:T(8,128)}, u32[]{:S(2)}) copy-start(f32[8,1,32,128]{3,2,1,0:T(8,128)} %convert_element_type.117) | copy-start | bytes 393220
  207.0 5.2 %copy-start.29 = (f32[8,1,32,128]{3,2,1,0:T(8,128)S(1)}, f32[8,1,32,128]{3,2,1,0:T(8,128)}, u32[]{:S(2)}) copy-start(f32[8,1,32,128]{3,2,1,0:T(8,128)} %convert_element_type.118) | copy-start | bytes 393220
  212.2 2.2 %copy-start.34 = (f32[2,16]{1,0:T(2,128)S(1)}, f32[2,16]{1,0:T(2,128)}, u32[]{:S(2)}) copy-start(f32[2,16]{1,0:T(2,128)} %copy-done.33) | copy-start | bytes 388
  212.2 2.2 %copy-start.37 = (pred[2,16]{1,0:T(4,128)(4,1)S(1)}, pred[2,16]{1,0:T(4,128)(4,1)}, u32[]{:S(2)}) copy-start(pred[2,16]{1,0:T(4,128)(4,1)} %fusion.64) | copy-start | bytes 100
  212.3 2.2 %copy-start.39 = (s32[2]{0:T(128)S(1)}, s32[2]{0:T(128)}, u32[]{:S(2)}) copy-start(s32[2]{0:T(128)} %iota_add_fusion) | copy-start | bytes 28
  212.3 2.5 %copy-start.22 = (bf16[2,32,512]{2,1,0:T(8,128)(2,1)S(1)}, bf16[2,32,512]{2,1,0:T(8,128)(2,1)}, u32[]{:S(2)}) copy-start(bf16[2,32,512]{2,1,0:T(8,128)(2,1)} %param.22) | copy-start | bytes 196612
  212.3 2.8 %copy-start.30 = (f32[32,1024]{1,0:T(8,128)S(1)}, f32[32,1024]{1,0:T(8,128)}, u32[]{:S(2)}) copy-start(f32[32,1024]{1,0:T(8,128)} %get-tuple-element.7) | copy-start | bytes 393220
  (1 other events, 1.6 us)
Sparse Core Ops, SparseCore 0:
  9.6 32.6 all-gather.3
  73.8 31.5 all-gather.5
  142.3 31.6 all-gather.7
where the time goes:
time: 225 us; the launch traced here: 223 us
  starting transfers between devices  67.1 us (30%)
  Pallas kernels  37 us (16%)
  local copies, waits for them, and re-layouts  26.6 us (12%)
  waiting for transfers between devices  25.6 us (11%)
  blocking collectives  23.8 us (11%)
  other arithmetic  19.4 us (9%)
  between operations  14.7 us (7%)
  matrix products  8.97 us (4%)
    ppermute x12, starting transfers between devices, faces(): return (lax.ppermute(last, axis, up), lax.ppermute(initial, axis, down))  40.9 us
    pallas_call x3, Pallas kernels, near_apply(): pl.pallas_call(near_kernel, out_shape=jax.ShapeDtypeStruct((exc, panels *...  23.8 us
    unnamed x89, local copies, waits for them, and re-layouts  20 us
    all_gather x2, blocking collectives, shards(): narrow = lax.all_gather(narrow, 'fem', axis=1, tiled=True)  13.6 us
    pallas_call x3, Pallas kernels, pick_nodes(): pl.pallas_call(pick_kernel, out_shape=jax.ShapeDtypeStruct((slots, x.shap...  13.2 us
    all_to_all x3, starting transfers between devices, shards(): lax.all_to_all(partial_sum.reshape(fem_count, share_cols, local_rows), 'f...  11.3 us
    all_to_all x1, blocking collectives, shards(): lax.all_to_all(outgoing.reshape(bem_count, CAP, excitations), 'bem', spli...  10.2 us
    all_to_all x2, starting transfers between devices, shards(): lax.all_to_all(outgoing.reshape(bem_count, CAP, excitations), 'bem', spli...  9.33 us
  transfers between devices with their start and end apart: 21, of which 7 were waited for; matrix products, arithmetic and copies ran while one was open for 12% of the time, Pallas kernels for 6%

commit v1 on v0

--- a/solution.py
+++ b/solution.py
@@ -1,3 +1,5 @@
+import functools
+
 import jax
 import jax.numpy as jnp
 from jax import lax
@@ -10,15 +12,99 @@
 
 
 HIGHEST = lax.Precision.HIGHEST
-
-
-def faces(x, axis, dim):
-    size, length = (lax.axis_size(axis), x.shape[dim])
-    up = [(i, (i + 1) % size) for i in range(size - 1)]
-    down = [(j, i) for i, j in up]
-    last = lax.slice_in_dim(x, length - 1, length, axis=dim).astype(jnp.bfloat16)
-    initial = lax.slice_in_dim(x, 0, 1, axis=dim).astype(jnp.bfloat16)
-    return lax.ppermute(last, axis, up), lax.ppermute(initial, axis, down)
+MESH = pl.DeviceIdType.MESH
+
+
+def exchange_kernel(plan, count, *refs):
+    items = len(plan)
+    sources, targets = refs[:items], refs[items : 2 * items]
+    send_sem, recv_sem, own_sem = refs[2 * items :]
+    sizes = {axis: lax.axis_size(axis) for axis in ("fem", "bem")}
+    ranks = {axis: lax.axis_index(axis) for axis in ("fem", "bem")}
+
+    def device(axis, step):
+        place = dict(ranks)
+        place[axis] = lax.rem(ranks[axis] + step, sizes[axis])
+        return (place["fem"], place["bem"])
+
+    def steps(kind, axis):
+        return [kind % sizes[axis]] if isinstance(kind, int) else range(1, sizes[axis])
+
+    peers = sorted({(axis, step) for kind, axis in plan for step in steps(kind, axis)})
+    barrier = pltpu.get_barrier_semaphore()
+    for axis, step in peers:
+        pl.semaphore_signal(barrier, inc=1, device_id=device(axis, step), device_id_type=MESH)
+    pl.semaphore_wait(barrier, len(peers))
+
+    def own_place(kind, axis, source, target):
+        rank = ranks[axis]
+        if kind == "gather":
+            rows = source.shape[1]
+            return target.at[:, pl.ds(pl.multiple_of(rank * rows, rows), rows), :]
+        return target.at[rank] if kind == "scatter" else target
+
+    copies = []
+    for (kind, axis), source, target in zip(plan, sources, targets):
+        for step in steps(kind, axis):
+            place = device(axis, step)
+            there = place[0] if axis == "fem" else place[1]
+            slot = len(copies)
+            copy = pltpu.make_async_remote_copy(
+                src_ref=source.at[there] if kind == "scatter" else source,
+                dst_ref=own_place(kind, axis, source, target),
+                send_sem=send_sem.at[slot],
+                recv_sem=recv_sem.at[slot],
+                device_id=place,
+                device_id_type=MESH,
+            )
+            copy.start()
+            copies.append(copy)
+    for item, ((kind, axis), source, target) in enumerate(zip(plan, sources, targets)):
+        if not isinstance(kind, int):
+            copy = pltpu.make_async_copy(
+                source.at[ranks[axis]] if kind == "scatter" else source,
+                own_place(kind, axis, source, target),
+                own_sem.at[item],
+            )
+            copy.start()
+            copies.append(copy)
+    for copy in copies:
+        copy.wait()
+
+
+def exchange(plan, arrays, name, collective_id):
+    shapes, count = [], 0
+    for (kind, axis), x in zip(plan, arrays):
+        size = lax.axis_size(axis)
+        count += 1 if isinstance(kind, int) else size - 1
+        shape = (x.shape[0], x.shape[1] * size, x.shape[2]) if kind == "gather" else x.shape
+        shapes.append(jax.ShapeDtypeStruct(shape, x.dtype))
+    return pl.pallas_call(
+        functools.partial(exchange_kernel, plan, count),
+        out_shape=shapes,
+        in_specs=[pl.BlockSpec(memory_space=pltpu.VMEM)] * len(arrays),
+        out_specs=[pl.BlockSpec(memory_space=pltpu.VMEM)] * len(arrays),
+        scratch_shapes=[
+            pltpu.SemaphoreType.DMA((count,)),
+            pltpu.SemaphoreType.DMA((count,)),
+            pltpu.SemaphoreType.DMA((len(plan),)),
+        ],
+        cost_estimate=pl.CostEstimate(
+            flops=1 << 29, bytes_accessed=sum(x.size for x in arrays) * 4, transcendentals=0
+        ),
+        compiler_params=pltpu.CompilerParams(
+            collective_id=collective_id, has_side_effects=True, vmem_limit_bytes=8 << 20
+        ),
+        name=name,
+    )(*arrays)
+
+
+def end_faces(state):
+    narrow = lambda x: x.astype(jnp.bfloat16)
+    return [narrow(state[-1:]), narrow(state[:1]), narrow(state[:, -1:]), narrow(state[:, :1])]
+
+
+FACE_PLAN = ((1, "fem"), (-1, "fem"), (1, "bem"), (-1, "bem"))
 
 
 def neighbour_sum(state, before_x, after_x, before_y, after_y):
@@ -40,9 +126,15 @@
     def _():
         acc_ref[...] = init_ref[...]
 
-    acc_ref[...] += jnp.dot(
-        x_ref[pairs_ref[p, k]], blocks_ref[0, 0], preferred_element_type=jnp.float32
-    )
+    width = blocks_ref.shape[1]
+    acc = acc_ref[...]
+    for i in range(width):
+        acc += jnp.dot(
+            x_ref[pairs_ref[p, k * width + i]],
+            blocks_ref[0, i],
+            preferred_element_type=jnp.float32,
+        )
+    acc_ref[...] = acc
 
     @pl.when(k == pl.num_programs(1) - 1)
     def _():
@@ -52,15 +144,16 @@
 def near_apply(pairs, x, blocks, init):
     panels, group, rows, cols = blocks.shape
     exc = x.shape[1]
+    width = next(w for w in (4, 3, 2, 1) if group % w == 0)
     return pl.pallas_call(
         near_kernel,
         out_shape=jax.ShapeDtypeStruct((exc, panels * cols), jnp.bfloat16),
         grid_spec=pltpu.PrefetchScalarGridSpec(
             num_scalar_prefetch=1,
-            grid=(panels, group),
+            grid=(panels, group // width),
             in_specs=[
                 pl.BlockSpec(x.shape, lambda p, k, pairs: (0, 0, 0)),
-                pl.BlockSpec((1, 1, rows, cols), lambda p, k, pairs: (p, k, 0, 0)),
+                pl.BlockSpec((1, width, rows, cols), lambda p, k, pairs: (p, k, 0, 0)),
                 pl.BlockSpec((exc, cols), lambda p, k, pairs: (0, p)),
             ],
             out_specs=pl.BlockSpec((exc, cols), lambda p, k, pairs: (0, p)),
@@ -70,7 +163,7 @@
             flops=2 * exc * blocks.size, bytes_accessed=2 * blocks.size, transcendentals=0
         ),
         compiler_params=pltpu.CompilerParams(
-            dimension_semantics=("arbitrary", "arbitrary"), vmem_limit_bytes=24 << 20
+            dimension_semantics=("arbitrary", "arbitrary"), vmem_limit_bytes=52 << 20
         ),
         name="near",
     )(pairs, x, blocks, init)
@@ -78,25 +171,23 @@
 
 def pick_kernel(node_ref, x_ref, out_ref):
     panels, exc, rows = x_ref.shape
-    slots = node_ref.shape[0]
+    slots = node_ref.shape[1]
     node = node_ref[...]
-    lanes = lax.broadcasted_iota(jnp.int32, (slots, rows), 1)
+    places = lax.broadcasted_iota(jnp.int32, (rows, slots), 0)
 
     def step(q, acc):
-        hot = jnp.where(lanes + q * rows == node, 1.0, 0.0).astype(jnp.bfloat16)
-        return acc + lax.dot_general(
-            hot, x_ref[q], (((1,), (1,)), ((), ())), preferred_element_type=jnp.float32
-        )
-
-    acc = lax.fori_loop(0, panels, step, jnp.zeros((slots, exc), jnp.float32))
+        hot = jnp.where(places == node - q * rows, 1.0, 0.0).astype(jnp.bfloat16)
+        return acc + jnp.dot(x_ref[q], hot, preferred_element_type=jnp.float32)
+
+    acc = lax.fori_loop(0, panels, step, jnp.zeros((exc, slots), jnp.float32), unroll=2)
     out_ref[...] = acc.astype(out_ref.dtype)
 
 
 def pick_nodes(node, x):
-    slots = node.shape[0]
+    slots = node.shape[1]
     return pl.pallas_call(
         pick_kernel,
-        out_shape=jax.ShapeDtypeStruct((slots, x.shape[1]), jnp.bfloat16),
+        out_shape=jax.ShapeDtypeStruct((x.shape[1], slots), jnp.bfloat16),
         cost_estimate=pl.CostEstimate(
             flops=2 * slots * x.size, bytes_accessed=2 * x.size, transcendentals=0
         ),
@@ -142,15 +233,13 @@
     places = jnp.arange(bem_count * CAP, dtype=jnp.int32)[:, None] == destination[None, :]
     send_rows = jnp.sum(jnp.where(places, trace_row[None, :] + 1, 0), axis=1) - 1
     send_cell = jnp.sum(jnp.where(places, trace_cell[None, :] + 1, 0), axis=1) - 1
-    recv_rows = lax.all_to_all(
-        send_rows.reshape(bem_count, CAP), "bem", split_axis=0, concat_axis=0, tiled=True
-    )
+    rows_wide = jnp.full((bem_count, 8, 128), -1, jnp.int32)
+    rows_wide = rows_wide.at[:, :, :CAP].set(send_rows.reshape(bem_count, 1, CAP))
     cell_ids = jnp.arange(cell_total, dtype=jnp.int32)
     send_hot = (send_cell[:, None] == cell_ids[None, :]).astype(jnp.bfloat16)
     cell_hot = (cell_ids[:, None] == trace_cell[None, :]).astype(jnp.bfloat16)
     row_ids = jnp.arange(local_rows, dtype=jnp.int32)
-    recv_hot = (recv_rows.reshape(-1)[:, None] == row_ids[None, :]).astype(jnp.bfloat16)
-    node = (slot_bank * local_rows + trace_row)[:, None]
+    node = (slot_bank * local_rows + trace_row)[None, :]
     own_first = bem_rank * local_panels
     own_centers = lax.dynamic_slice_in_dim(centers, own_first, local_panels, 0)
     offsets = own_centers[:, None, :] - centers[None, :, :]
@@ -171,22 +260,27 @@
         narrow = whole.astype(jnp.bfloat16).reshape(-1, local_panels, panel_rows)
         narrow = jnp.transpose(narrow, (1, 0, 2))
         if sweep > 0:
-            narrow = lax.all_gather(narrow, "fem", axis=1, tiled=True)
+            (narrow,) = exchange((("gather", "fem"),), [narrow], "share_gather", 1)
         x = lax.all_gather(narrow, "bem", axis=0, tiled=True)
-        before_x, after_x = faces(fem_state, "fem", 0)
-        before_y, after_y = faces(fem_state, "bem", 1)
         outgoing = jnp.dot(
             send_hot,
             fem_state.astype(jnp.bfloat16).reshape(cell_total, excitations),
             preferred_element_type=jnp.float32,
         ).astype(jnp.bfloat16)
-        incoming = lax.all_to_all(
-            outgoing.reshape(bem_count, CAP, excitations),
-            "bem",
-            split_axis=0,
-            concat_axis=0,
-            tiled=True,
-        )
+        arrays = [*end_faces(fem_state), outgoing.reshape(bem_count, CAP, excitations)]
+        plan = (*FACE_PLAN, ("scatter", "bem"))
+        if sweep == 0:
+            *layers, incoming, recv_rows = exchange(
+                (*plan, ("scatter", "bem")), [*arrays, rows_wide], "first_exchange", 0
+            )
+            recv_rows = recv_rows[:, 0, :CAP].reshape(-1)
+            recv_hot = (recv_rows[:, None] == row_ids[None, :]).astype(jnp.bfloat16)
+        else:
+            *layers, incoming = exchange(plan, arrays, "layer_exchange", 2)
+        inside = (fem_rank > 0, fem_rank < fem_count - 1, bem_rank > 0, bem_rank < bem_count - 1)
+        layers = [
+            jnp.where(here, x, jnp.zeros_like(x)) for here, x in zip(inside, layers)
+        ]
         traced = lax.dot_general(
             incoming.reshape(-1, excitations),
             recv_hot,
@@ -194,12 +288,11 @@
             preferred_element_type=jnp.float32,
         )
         partial_sum = near_apply(pair_group, x, near_blocks, traced)
-        parts = lax.all_to_all(
-            partial_sum.reshape(fem_count, share_cols, local_rows),
-            "fem",
-            split_axis=0,
-            concat_axis=0,
-            tiled=True,
+        (parts,) = exchange(
+            (("scatter", "fem"),),
+            [partial_sum.reshape(fem_count, share_cols, local_rows)],
+            "part_scatter",
+            3,
         )
         own_cols = lax.dynamic_slice_in_dim(x, first_col, share_cols, 1)
         reduced = jnp.einsum(
@@ -211,11 +304,11 @@
             share_cols, local_rows
         )
         values = pick_nodes(node, x)
-        coupled = jnp.dot(cell_hot, values, preferred_element_type=jnp.float32).reshape(
-            fem_state.shape
-        )
+        coupled = lax.dot_general(
+            cell_hot, values, (((1,), (1,)), ((), ())), preferred_element_type=jnp.float32
+        ).reshape(fem_state.shape)
         scale = (6.0 + reaction)[..., None]
-        beside = neighbour_sum(fem_state, before_x, after_x, before_y, after_y)
+        beside = neighbour_sum(fem_state, *layers)
         fem_next = fem_state + (fem_source - (scale * fem_state - beside) - coupled) / scale
         applied = distant + jnp.sum(parts.astype(jnp.float32), axis=0)
         density = density + (source_part - applied) / diag_row

time: 225 us -> 179 us (0.80)
  starting transfers between devices: 67.1 us -> 0.12 us
  Pallas kernels: 37 us -> 91.3 us
  waiting for transfers between devices: 25.6 us -> 51.5 us
  local copies, waits for them, and re-layouts: 26.6 us -> 2.71 us
  blocking collectives: 23.8 us -> 0 us
  other arithmetic: 19.4 us -> 10.2 us
  matrix products: 8.97 us -> 6.21 us
    pallas_call x3 -> x11, Pallas kernels: 13.2 us -> 66.2 us  [the longest x8 60.3 us: exchange(): pl.pallas_call(functools.partial(exchange_kernel, plan, count), out_shape...]
    all_gather x3, waiting for transfers between devices: 8.03 us -> 51.5 us  [shards(): x = lax.all_gather(narrow, 'bem', axis=0, tiled=True)]
    ppermute x12 -> x0, starting transfers between devices: 40.9 us -> none  [faces(): return (lax.ppermute(last, axis, up), lax.ppermute(initial, axis, down))]
    all_to_all x6 -> x0, starting transfers between devices: 26.2 us -> none  [the longest x3 11.3 us: shards(): lax.all_to_all(partial_sum.reshape(fem_count, share_cols, local_rows), 'f...]
    unnamed x89 -> x37, local copies, waits for them, and re-layouts: 20 us -> 1.42 us
    all_gather x2 -> x0, blocking collectives: 13.6 us -> none  [shards(): narrow = lax.all_gather(narrow, 'fem', axis=1, tiled=True)]
    all_to_all x6 -> x0, waiting for transfers between devices: 12.1 us -> none  [the longest x2 5.03 us: shards(): lax.all_to_all(outgoing.reshape(bem_count, CAP, excitations), 'bem', spli...]
    all_to_all x1 -> x0, blocking collectives: 10.2 us -> none  [shards(): lax.all_to_all(outgoing.reshape(bem_count, CAP, excitations), 'bem', spli...]
  transfers between devices with their start and end apart: 21 -> 3, of which waited for: 7 -> 3; matrix products, arithmetic and copies ran while one was open for 12% -> 5% of each run, Pallas kernels for 6% -> 21%
where the time goes in v1:
time: 179 us; the launch traced here: 177 us
  Pallas kernels  91.3 us (51%)
  waiting for transfers between devices  51.5 us (29%)
  between operations  14.5 us (8%)
  other arithmetic  10.2 us (6%)
  matrix products  6.21 us (3%)
  local copies, waits for them, and re-layouts  2.71 us (2%)
    pallas_call x8, Pallas kernels, exchange(): pl.pallas_call(functools.partial(exchange_kernel, plan, count), out_shape...  60.3 us
    all_gather x3, waiting for transfers between devices, shards(): x = lax.all_gather(narrow, 'bem', axis=0, tiled=True)  51.5 us
    pallas_call x3, Pallas kernels, near_apply(): pl.pallas_call(near_kernel, out_shape=jax.ShapeDtypeStruct((exc, panels *...  25.1 us
    pallas_call x3, Pallas kernels, pick_nodes(): pl.pallas_call(pick_kernel, out_shape=jax.ShapeDtypeStruct((x.shape[1], s...  5.9 us
  transfers between devices with their start and end apart: 3, of which 3 were waited for; matrix products, arithmetic and copies ran while one was open for 5% of the time, Pallas kernels for 21%

profile of v1, /device:TPU:3, one launch (start us, length us, event | category | flops | bytes accessed | tf_op | source)
XLA Modules:
  0.0 176.5 jit_solution(7080492815570011900)
XLA Ops:
  7.2 0.0 copy-start
  7.2 0.0 copy-start.8
  7.2 0.0 all-gather.4.cloned.1.call-start
  7.3 1.3 copy.42
  8.6 0.9 copy.43
  9.4 0.0 all-gather.4.cloned.1.call-update
  9.5 0.0 all-gather.6.cloned.1.call-start
  9.5 0.1 convert.18
  9.6 0.0 copy-start.16
  9.6 0.0 copy-start.15
  9.7 0.2 convert_reduce_fusion.3
  9.9 0.2 select_reduce_fusion
  10.1 0.1 sub.59
  10.2 0.5 fusion.6
  10.7 9.3 %first_exchange.1 = (bf16[1,8,32,128]{3,2,1,0:T(8,128)(2,1)S(1)}, bf16[1,8,32,128]{3,2,1,0:T(8,128)(2,1)S(1)}, bf16[8,1,32,128]{3,2,1,0:T(8,128)(2,1)S(1)}, bf16...) custom-call(bf16[1,8,32,128]{3,2,1,0:T(8,128)(2,1)S(1)} %get-tuple-element.67.refs_0_, ...), custom_call_target="tpu_custom_call" | custom-call | flops 536870912 | bytes 688128 | tf_op jit(solution)/shard_map/first_exchange/pallas_call | solution.py:82
  20.0 0.1 eq.114
  20.1 0.1 constant_dynamic-slice_fusion.pairs_ref
  20.2 0.1 constant_dynamic-slice_fusion.1
  20.3 0.1 fusion.64
  20.4 0.1 multiply_reduce_fusion
  20.5 0.4 fusion.41.init_ref
  20.9 20.2 %all-gather.4.cloned.1.call-done.x_ref = bf16[16,128,512]{2,1,0:T(8,128)(2,1)} async-done(((bf16[2,128,512]{2,1,0:T(8,128)(2,1)}), bf16[16,128,512]{2,1,0:T(8,128)(2,1)}) %all-gather.4.cloned.1.call-update) | async-done | bytes 2097168 | tf_op jit(solution)/shard_map/all_gather | solution.py:264
  41.1 8.4 %near.3 = bf16[128,1024]{1,0:T(8,128)(2,1)S(1)} custom-call(s32[2,12]{1,0:T(2,128)S(1)} %constant_dynamic-slice_fusion.pairs_ref, bf16[16,128,512]{2,1,0:T(8,128)(2,1)} %all-gather.4.cloned.1.call-done.x_ref, bf16[2,12,512,512]{3,2,1,0:T(8,128)(2,1)} %blocks_ref.5, f32[128,1024]{1,0:T(8,128)S(1)} %fusion.41.init_ref), custom_call_target="tpu_custom_call" | custom-call | flops 1610612736 | bytes 12582912 | tf_op jit(solution)/shard_map/near/pallas_call | solution.py:148
  49.5 0.0 copy-start.10
  49.5 5.5 %part_scatter.3 = bf16[4,32,1024]{2,1,0:T(8,128)(2,1)S(1)} custom-call(bf16[4,32,1024]{2,1,0:T(8,128)(2,1)S(1)} %bitcast.69), custom_call_target="tpu_custom_call" | custom-call | flops 536870912 | bytes 524288 | tf_op jit(solution)/shard_map/part_scatter/pallas_call | solution.py:82
  55.0 0.3 convolution_convert_fusion.2
  55.3 0.0 copy-start.12
  55.3 0.3 fusion.59
  55.6 0.2 convolution_bitcast_fusion.2
  55.8 1.0 fusion.76
  56.8 5.6 %share_gather.2 = bf16[2,128,512]{2,1,0:T(8,128)(2,1)} custom-call(bf16[2,32,512]{2,1,0:T(8,128)(2,1)S(1)} %bitcast.74), custom_call_target="tpu_custom_call" | custom-call | flops 536870912 | bytes 131072 | tf_op jit(solution)/shard_map/share_gather/pallas_call | solution.py:82
  62.4 0.0 all-gather.6.cloned.1.call-update
  62.4 0.0 all-gather.8.cloned.1.call-start
  62.7 2.0 %pick.3 = bf16[128,256]{1,0:T(8,128)(2,1)S(1)} custom-call(s32[1,256]{1,0:T(1,128)S(1)} %bitcast.76, bf16[16,128,512]{2,1,0:T(8,128)(2,1)S(1)} %copy-done.1), custom_call_target="tpu_custom_call" | custom-call | flops 536870912 | bytes 2097152 | tf_op jit(solution)/shard_map/pick/pallas_call | solution.py:188
  64.6 0.5 fusion.2
  65.1 2.1 %fusion.74 = (bf16[8,8,32,128]{3,2,1,0:T(8,128)(2,1)S(1)}, f32[8,8,32,128]{3,2,1,0:T(8,128)}) fusion(f32[8,8,32,128]{3,2,1,0:T(8,128)S(1)} %copy-done.9, f32[8,8,32,128]{3,2,1,0:T(8,128)S(1)} %bitcast.83, f32[8,8,32,128]{3,2,1,0:T(8,128)S(1)} %copy-done.4, f32[8,1,32,128]{3,2,1,0:T(8,128)S(1)} %select_convert_fusion.8, ...), kind=kLoop, calls=%fused_computation.139 | loop fusion | flops 4194304 | bytes 5251072 | tf_op jit(solution)/shard_map/convert.7
  67.3 0.5 fusion.7
  67.8 12.8 %layer_exchange.2 = (bf16[1,8,32,128]{3,2,1,0:T(8,128)(2,1)S(1)}, bf16[1,8,32,128]{3,2,1,0:T(8,128)(2,1)S(1)}, bf16[8,1,32,128]{3,2,1,0:T(8,128)(2,1)S(1)}, bf16...) custom-call(bf16[1,8,32,128]{3,2,1,0:T(8,128)(2,1)S(1)} %get-tuple-element.63.refs_0_, ...), custom_call_target="tpu_custom_call" | custom-call | flops 536870912 | bytes 655360 | tf_op jit(solution)/shard_map/layer_exchange/pallas_call | solution.py:82
  80.6 0.4 fusion.40.init_ref
  81.0 14.8 %all-gather.6.cloned.1.call-done.x_ref = bf16[16,128,512]{2,1,0:T(8,128)(2,1)} async-done(((bf16[2,128,512]{2,1,0:T(8,128)(2,1)}), bf16[16,128,512]{2,1,0:T(8,128)(2,1)}) %all-gather.6.cloned.1.call-update) | async-done | bytes 2097168 | tf_op jit(solution)/shard_map/all_gather | solution.py:264
  95.7 8.4 %near.4 = bf16[128,1024]{1,0:T(8,128)(2,1)S(1)} custom-call(s32[2,12]{1,0:T(2,128)S(1)} %constant_dynamic-slice_fusion.pairs_ref, bf16[16,128,512]{2,1,0:T(8,128)(2,1)} %all-gather.6.cloned.1.call-done.x_ref, bf16[2,12,512,512]{3,2,1,0:T(8,128)(2,1)} %blocks_ref.5, f32[128,1024]{1,0:T(8,128)S(1)} %fusion.40.init_ref), custom_call_target="tpu_custom_call" | custom-call | flops 1610612736 | bytes 12582912 | tf_op jit(solution)/shard_map/near/pallas_call | solution.py:148
  104.1 5.5 %part_scatter.4 = bf16[4,32,1024]{2,1,0:T(8,128)(2,1)S(1)} custom-call(bf16[4,32,1024]{2,1,0:T(8,128)(2,1)S(1)} %bitcast.70), custom_call_target="tpu_custom_call" | custom-call | flops 536870912 | bytes 524288 | tf_op jit(solution)/shard_map/part_scatter/pallas_call | solution.py:82
  109.6 0.3 convolution_convert_fusion.1
  109.9 0.3 fusion.57
  110.2 0.2 convolution_bitcast_fusion.1
  110.4 1.0 fusion.73
  111.4 5.6 %share_gather.3 = bf16[2,128,512]{2,1,0:T(8,128)(2,1)} custom-call(bf16[2,32,512]{2,1,0:T(8,128)(2,1)S(1)} %bitcast.75), custom_call_target="tpu_custom_call" | custom-call | flops 536870912 | bytes 131072 | tf_op jit(solution)/shard_map/share_gather/pallas_call | solution.py:82
  117.0 0.0 all-gather.8.cloned.1.call-update
  117.1 2.0 %pick.4 = bf16[128,256]{1,0:T(8,128)(2,1)S(1)} custom-call(s32[1,256]{1,0:T(1,128)S(1)} %bitcast.77, bf16[16,128,512]{2,1,0:T(8,128)(2,1)S(1)} %copy-done.2), custom_call_target="tpu_custom_call" | custom-call | flops 536870912 | bytes 2097152 | tf_op jit(solution)/shard_map/pick/pallas_call | solution.py:188
  119.1 0.5 fusion.1
  119.6 1.3 fusion.71
  120.9 0.5 fusion.8
  121.4 10.6 %layer_exchange.3 = (bf16[1,8,32,128]{3,2,1,0:T(8,128)(2,1)S(1)}, bf16[1,8,32,128]{3,2,1,0:T(8,128)(2,1)S(1)}, bf16[8,1,32,128]{3,2,1,0:T(8,128)(2,1)S(1)}, bf16...) custom-call(bf16[1,8,32,128]{3,2,1,0:T(8,128)(2,1)S(1)} %get-tuple-element.59.refs_0_, ...), custom_call_target="tpu_custom_call" | custom-call | flops 536870912 | bytes 655360 | tf_op jit(solution)/shard_map/layer_exchange/pallas_call | solution.py:82
  132.1 0.4 fusion.39.init_ref
  132.5 16.5 %all-gather.8.cloned.1.call-done.x_ref = bf16[16,128,512]{2,1,0:T(8,128)(2,1)} async-done(((bf16[2,128,512]{2,1,0:T(8,128)(2,1)}), bf16[16,128,512]{2,1,0:T(8,128)(2,1)}) %all-gather.8.cloned.1.call-update) | async-done | bytes 2097168 | tf_op jit(solution)/shard_map/all_gather | solution.py:264
  149.0 8.4 %near.5 = bf16[128,1024]{1,0:T(8,128)(2,1)S(1)} custom-call(s32[2,12]{1,0:T(2,128)S(1)} %constant_dynamic-slice_fusion.pairs_ref, bf16[16,128,512]{2,1,0:T(8,128)(2,1)} %all-gather.8.cloned.1.call-done.x_ref, bf16[2,12,512,512]{3,2,1,0:T(8,128)(2,1)} %blocks_ref.5, f32[128,1024]{1,0:T(8,128)S(1)} %fusion.39.init_ref), custom_call_target="tpu_custom_call" | custom-call | flops 1610612736 | bytes 12582912 | tf_op jit(solution)/shard_map/near/pallas_call | solution.py:148
  157.4 5.5 %part_scatter.5 = bf16[4,32,1024]{2,1,0:T(8,128)(2,1)S(1)} custom-call(bf16[4,32,1024]{2,1,0:T(8,128)(2,1)S(1)} %bitcast.68), custom_call_target="tpu_custom_call" | custom-call | flops 536870912 | bytes 524288 | tf_op jit(solution)/shard_map/part_scatter/pallas_call | solution.py:82
  163.0 0.3 convolution_convert_fusion
  163.3 0.3 fusion.55
  163.5 0.2 convolution_bitcast_fusion
  163.8 2.0 %pick.5 = bf16[128,256]{1,0:T(8,128)(2,1)S(1)} custom-call(s32[1,256]{1,0:T(1,128)S(1)} %bitcast.78, bf16[16,128,512]{2,1,0:T(8,128)(2,1)S(1)} %copy-done.3), custom_call_target="tpu_custom_call" | custom-call | flops 536870912 | bytes 2097152 | tf_op jit(solution)/shard_map/pick/pallas_call | solution.py:188
  165.7 0.5 fusion
  166.2 1.6 divide_add_fusion
  167.8 2.2 %fusion.29 = f32[8,8,32,128]{3,2,1,0:T(8,128)} fusion(f32[8,8,32,128]{3,2,1,0:T(8,128)S(1)} %get-tuple-element.49, f32[8,8,32,128]{3,2,1,0:T(8,128)S(1)} %bitcast.84, f32[8,8,32,128]{3,2,1,0:T(8,128)S(1)} %copy-done.6, f32[8,1,32,128]{3,2,1,0:T(8,128)S(1)} %select_convert_fusion, f32[8,1,32,128]{3,2,1,0:T(8,128)S(1)} %select_convert_fusion.1, ...), kind=kLoop, calls=%fused_computation.43 | loop fusion | flops 3932160 | bytes 4726784 | tf_op jit(solution)/shard_map/add | solution.py:312
  (64 shorter events, 0.5 us)
Async XLA Ops:
  7.2 47.8 %copy-start = (bf16[16,32,512]{2,1,0:T(8,128)(2,1)S(1)}, bf16[16,32,512]{2,1,0:T(8,128)(2,1)}, u32[]{:S(2)}) copy-start(bf16[16,32,512]{2,1,0:T(8,128)(2,1)} %param.25) | copy-start | bytes 1572868
  7.2 2.3 %copy-start.8 = (f32[8,8,32,128]{3,2,1,0:T(8,128)S(1)}, f32[8,8,32,128]{3,2,1,0:T(8,128)}, u32[]{:S(2)}) copy-start(f32[8,8,32,128]{3,2,1,0:T(8,128)} %param.16) | copy-start | bytes 3145732
  7.2 2.5 %copy-start.14 = (s32[256,1]{0,1:T(1,128)S(1)}, s32[256,1]{0,1:T(1,128)}, u32[]{:S(2)}) copy-start(s32[256,1]{0,1:T(1,128)} %param.28) | copy-start | bytes 3076
  7.2 2.6 %copy-start.13 = (s32[256]{0:T(256)S(1)}, s32[256]{0:T(256)}, u32[]{:S(2)}) copy-start(s32[256]{0:T(256)} %param.27) | copy-start | bytes 3076
  7.2 2.6 %copy-start.17 = (s32[256]{0:T(256)S(1)}, s32[256]{0:T(256)}, u32[]{:S(2)}) copy-start(s32[256]{0:T(256)} %param.29) | copy-start | bytes 3076
  7.2 33.9 %all-gather.4.cloned.1.call-start = ((), (), s32[]{:S(2)}) async-start(), calls=%async_computation | async-start | bytes 2359296 | tf_op jit(solution)/shard_map/all_gather | solution.py:264
  9.5 86.3 %all-gather.6.cloned.1.call-start = ((), (), s32[]{:S(2)}) async-start(), calls=%async_computation.1 | async-start | bytes 2359296 | tf_op jit(solution)/shard_map/all_gather | solution.py:264
  9.6 10.5 %copy-start.16 = (s32[2,48]{1,0:T(2,128)S(1)}, s32[2,48]{1,0:T(2,128)}, u32[]{:S(2)}) copy-start(s32[2,48]{1,0:T(2,128)} %param.23) | copy-start | bytes 1156
  9.6 10.5 %copy-start.15 = (f32[16,3]{0,1:T(4,128)S(1)}, f32[16,3]{0,1:T(4,128)}, u32[]{:S(2)}) copy-start(f32[16,3]{0,1:T(4,128)} %param.26) | copy-start | bytes 580
  49.4 5.6 %copy-start.1 = (bf16[16,128,512]{2,1,0:T(8,128)(2,1)S(1)}, bf16[16,128,512]{2,1,0:T(8,128)(2,1)}, u32[]{:S(2)}) copy-start(bf16[16,128,512]{2,1,0:T(8,128)(2,1)} %all-gather.4.cloned.1.call-done.x_ref) | copy-start | bytes 6291460
  49.5 6.1 %copy-start.10 = (bf16[2,32,512]{2,1,0:T(8,128)(2,1)S(1)}, bf16[2,32,512]{2,1,0:T(8,128)(2,1)}, u32[]{:S(2)}) copy-start(bf16[2,32,512]{2,1,0:T(8,128)(2,1)} %param.24) | copy-start | bytes 196612
  49.5 6.3 %copy-start.11 = (f32[1024]{0:T(1024)S(1)}, f32[1024]{0:T(1024)}, u32[]{:S(2)}) copy-start(f32[1024]{0:T(1024)} %param.21) | copy-start | bytes 12292
  55.3 7.2 %copy-start.12 = (f32[8,8,32]{2,1,0:T(8,128)S(1)}, f32[8,8,32]{2,1,0:T(8,128)}, u32[]{:S(2)}) copy-start(f32[8,8,32]{2,1,0:T(8,128)} %param.18) | copy-start | bytes 24580
  62.4 86.6 %all-gather.8.cloned.1.call-start = ((), (), s32[]{:S(2)}) async-start(), calls=%async_computation.2 | async-start | bytes 2359296 | tf_op jit(solution)/shard_map/all_gather | solution.py:264
  62.5 2.6 %copy-start.4 = (f32[8,8,32,128]{3,2,1,0:T(8,128)S(1)}, f32[8,8,32,128]{3,2,1,0:T(8,128)}, u32[]{:S(2)}) copy-start(f32[8,8,32,128]{3,2,1,0:T(8,128)} %param.17) | copy-start | bytes 3145732
  62.5 2.6 %copy-start.9 = (f32[8,8,32,128]{3,2,1,0:T(8,128)S(1)}, f32[8,8,32,128]{3,2,1,0:T(8,128)}, u32[]{:S(2)}) copy-start(f32[8,8,32,128]{3,2,1,0:T(8,128)} %param.16) | copy-start | bytes 3145732
  104.1 5.5 %copy-start.2 = (bf16[16,128,512]{2,1,0:T(8,128)(2,1)S(1)}, bf16[16,128,512]{2,1,0:T(8,128)(2,1)}, u32[]{:S(2)}) copy-start(bf16[16,128,512]{2,1,0:T(8,128)(2,1)} %all-gather.6.cloned.1.call-done.x_ref) | copy-start | bytes 6291460
  117.0 2.6 %copy-start.5 = (f32[8,8,32,128]{3,2,1,0:T(8,128)S(1)}, f32[8,8,32,128]{3,2,1,0:T(8,128)}, u32[]{:S(2)}) copy-start(f32[8,8,32,128]{3,2,1,0:T(8,128)} %param.17) | copy-start | bytes 3145732
  117.0 2.6 %copy-start.7 = (f32[8,8,32,128]{3,2,1,0:T(8,128)S(1)}, f32[8,8,32,128]{3,2,1,0:T(8,128)}, u32[]{:S(2)}) copy-start(f32[8,8,32,128]{3,2,1,0:T(8,128)} %get-tuple-element.53) | copy-start | bytes 3145732
  157.4 5.5 %copy-start.3 = (bf16[16,128,512]{2,1,0:T(8,128)(2,1)S(1)}, bf16[16,128,512]{2,1,0:T(8,128)(2,1)}, u32[]{:S(2)}) copy-start(bf16[16,128,512]{2,1,0:T(8,128)(2,1)} %all-gather.8.cloned.1.call-done.x_ref) | copy-start | bytes 6291460
  163.7 4.1 %copy-start.6 = (f32[8,8,32,128]{3,2,1,0:T(8,128)S(1)}, f32[8,8,32,128]{3,2,1,0:T(8,128)}, u32[]{:S(2)}) copy-start(f32[8,8,32,128]{3,2,1,0:T(8,128)} %param.17) | copy-start | bytes 3145732
Sparse Core Ops, SparseCore 0:
  10.2 30.8 all-gather.3
  62.6 33.1 all-gather.5
  117.1 31.8 all-gather.7
